TPU v7x, 32 devices: a whole 2x2x4 slice. The times are simulated.
32 devices in a mesh: ep: 8 (over z, y), tp: 4 (over x, core).
Axes of the slice: x: 2, y: 2, z: 4, core: 2. Of those that a mesh axis runs over, the one named last changes fastest.
Arguments:
- tokens: bfloat16 [512, 4096], P(('ep', 'tp')), may hold values from -6 to 6
- routes: int32 [512, 2], P(('ep', 'tp')), may hold values from 0 to 7, all different within a row; in each aligned block of 16 rows (0 to 15, 16 to 31, ...) at most 8 rows name the same one
- combine: float32 [512, 2], P(('ep', 'tp')), may hold values from 0.25 to 1
- gate_weight: bfloat16 [8, 4096, 4096], P('ep', None, 'tp'), may hold values from -0.09375 to 0.09375
- up_weight: bfloat16 [8, 4096, 4096], P('ep', None, 'tp'), may hold values from -0.09375 to 0.09375
- down_weight: bfloat16 [8, 4096, 4096], P('ep', 'tp'), may hold values from -0.09375 to 0.09375
Outputs:
- moe_output: bfloat16 [512, 4096], P(('ep', 'tp'))
Inputs may be any that keep to these rules, and one draw needn't show every extreme that they name: `routes`: each row names 2 different experts. Among the rows of one device no expert is named more than 8 times, and in every draw some expert is named exactly 8 times by the rows of some device.
All inputs are finite; a program needn't handle non-finite values.
Results may differ from a plain program's by a relative error of at most 0.015.
Values may be sent and summed in bfloat16 or wider, within the bound.
A program may use at most 64 MiB of HBM per device.

v0:
```python
import jax
import jax.numpy as jnp
from jax import lax
from jax.sharding import PartitionSpec as P


def body(tokens, routes, combine, gate_weight, up_weight, down_weight):
    token_rows, feature_width = tokens.shape
    top_count = routes.shape[1]
    experts_here = gate_weight.shape[0]
    rank_count = lax.axis_size("ep")
    experts_all = experts_here * rank_count
    capacity = 2 * token_rows * top_count // experts_all
    flat_ids = routes.reshape(-1)
    onehot = (flat_ids[:, None] == jnp.arange(experts_all, dtype=jnp.int32)[None, :]).astype(
        jnp.int32
    )
    earlier = jnp.cumsum(onehot, axis=0) - onehot
    slot_index = jnp.sum(earlier * onehot, axis=1)
    target = flat_ids * capacity + slot_index
    selector = (
        target[:, None] == jnp.arange(experts_all * capacity, dtype=jnp.int32)[None, :]
    ).astype(jnp.bfloat16)
    repeated = jnp.repeat(tokens, top_count, axis=0)
    buffer = lax.dot_general(
        selector, repeated, (((0,), (0,)), ((), ())), preferred_element_type=jnp.float32
    ).astype(jnp.bfloat16)
    shaped = buffer.reshape(rank_count, 1, experts_here, capacity, feature_width)
    arrived = lax.all_to_all(shaped, "ep", split_axis=0, concat_axis=0, tiled=True)
    block_rows = lax.all_gather(arrived, "tp", axis=1, tiled=True)
    gate_values = jnp.einsum(
        "abecd,edf->abecf", block_rows, gate_weight, preferred_element_type=jnp.float32
    )
    up_values = jnp.einsum(
        "abecd,edf->abecf", block_rows, up_weight, preferred_element_type=jnp.float32
    )
    hidden = (jax.nn.silu(gate_values) * up_values).astype(jnp.bfloat16)
    partials = jnp.einsum(
        "abecf,efd->abecd", hidden, down_weight, preferred_element_type=jnp.float32
    )
    summed = lax.psum_scatter(partials.astype(jnp.bfloat16), "tp", scatter_dimension=1, tiled=True)
    returned = lax.all_to_all(summed, "ep", split_axis=0, concat_axis=0, tiled=True)
    returned = returned.reshape(experts_all * capacity, feature_width)
    picked = jnp.dot(selector, returned, preferred_element_type=jnp.float32).reshape(
        token_rows, top_count, feature_width
    )
    return jnp.sum(combine[:, :, None] * picked, axis=1).astype(jnp.bfloat16)


def solution(mesh):
    return jax.shard_map(
        body,
        mesh=mesh,
        in_specs=(
            P(("ep", "tp"), None),
            P(("ep", "tp"), None),
            P(("ep", "tp"), None),
            P("ep", None, "tp"),
            P("ep", None, "tp"),
            P("ep", "tp", None),
        ),
        out_specs=P(("ep", "tp"), None),
        check_vma=False,
    )
```

profile of v0, /device:TPU:0, one launch (start us, length us, event | category | flops | bytes accessed | tf_op | source)
XLA Modules:
  0.0 152.7 jit_solution(6297224300718134010)
XLA Ops:
  6.5 0.8 copy.24
  7.3 0.1 eq.50
  7.4 0.1 fusion.52
  7.5 0.1 reduce_window_sum.11
  7.5 0.2 select_reduce_fusion
  7.7 1.1 broadcast_in_dim.2
  8.8 0.1 reshape.65
  8.9 0.4 fusion.12
  9.3 21.7 %all_to_all.10 = bf16[8,1,1,8,4096]{4,3,1,2,0:T(8,128)(2,1)} all-to-all(bf16[8,1,1,8,4096]{4,3,1,2,0:T(8,128)(2,1)S(1)} %fusion.12), channel_id=1, replica_groups=mesh['ep'=8,'tp'=4] {'ep'}, dimensions={0} | all-to-all | bytes 1048576 | tf_op jit(solution)/shard_map/all_to_all | solution.py:29
  31.1 0.0 all-gather.2.cloned.1.call-update
  31.1 0.0 all-reduce.3.cloned.1.call-start
  31.2 21.7 %all-gather.2.cloned.1.call-done = bf16[8,4,1,8,4096]{4,3,1,0,2:T(8,128)(2,1)} async-done(((bf16[8,1,1,8,4096]{4,3,1,0,2:T(8,128)(2,1)}), bf16[8,4,1,8,4096]{4,3,1,0,2:T(8,128)(2,1)}) %all-gather.2.cloned.1.call-update) | async-done | bytes 2097168 | tf_op jit(solution)/shard_map/all_gather | solution.py:30
  52.8 6.5 %fusion.15 = f32[8,4,1,8,1024]{4,3,1,0,2:T(8,128)S(1)} fusion(bf16[1,4096,1024]{2,1,0:T(8,128)(2,1)} %param.9, bf16[8,4,1,8,4096]{4,3,1,0,2:T(8,128)(2,1)} %all-gather.2.cloned.1.call-done), kind=kOutput, calls=%fused_computation.13 | convolution fusion | flops 2147483648 | bytes 11534336 | tf_op jit(solution)/shard_map/abecd,edf->abecf/dot_general | solution.py:31
  59.3 0.0 copy-start.3
  59.4 11.7 %fusion.9 = bf16[8,4,1,8,4096]{4,3,1,0,2:T(8,128)(2,1)} fusion(bf16[1,1024,4096]{2,1,0:T(8,128)(2,1)} %param.11, bf16[1,4096,1024]{2,1,0:T(8,128)(2,1)} %param.10, bf16[8,4,1,8,4096]{4,3,1,0,2:T(8,128)(2,1)S(1)} %copy-done.2, f32[8,4,1,8,1024]{4,3,1,0,2:T(8,128)S(1)} %fusion.15), kind=kOutput, calls=%fused_computation.7 | convolution fusion | flops 4297588736 | bytes 22020096 | tf_op jit(solution)/shard_map/abecf,efd->abecd/dot_general | solution.py:38
  71.0 0.0 all-reduce.3.cloned.1.call-update
  71.1 0.6 dynamic-slice
  71.7 50.9 %all-reduce.3.cloned.1.call-done = bf16[8,4,1,8,4096]{4,3,1,0,2:T(8,128)(2,1)} async-done(((bf16[8,4,1,8,4096]{4,3,1,0,2:T(8,128)(2,1)}), bf16[8,4,1,8,4096]{4,3,1,0,2:T(8,128)(2,1)}) %all-reduce.3.cloned.1.call-update) | async-done | bytes 2097168
  122.6 2.5 %dynamic-slice_bitcast_fusion = bf16[8,1,1,8,4096]{4,3,1,2,0:T(8,128)(2,1)} fusion(bf16[8,4,1,8,4096]{4,3,1,0,2:T(8,128)(2,1)} %all-reduce.3.cloned.1.call-done, u32[]{:T(128)} %bitcast.44), kind=kLoop, calls=%fused_computation.25 | loop fusion | bytes 1048580 | tf_op jit(solution)/shard_map/reduce_scatter | solution.py:41
  125.1 5.5 %all-to-all-start.1 = ((bf16[8,1,1,8,4096]{4,3,1,2,0:T(8,128)(2,1)}), bf16[8,1,1,8,4096]{4,3,1,2,0:T(8,128)(2,1)S(1)}, u32[]{:S(2)}, u32[]{:S(2)}) async-start(bf16[8,1,1,8,4096]{4,3,1,2,0:T(8,128)(2,1)} %dynamic-slice_bitcast_fusion), calls=%async_computation.1 | async-start | bytes 1048576 | tf_op jit(solution)/shard_map/all_to_all | solution.py:42
  130.6 0.1 reduce_sum.21
  130.7 0.1 copy.25
  130.8 14.1 %all-to-all-done.1 = bf16[8,1,1,8,4096]{4,3,1,2,0:T(8,128)(2,1)S(1)} async-done(((bf16[8,1,1,8,4096]{4,3,1,2,0:T(8,128)(2,1)}), bf16[8,1,1,8,4096]{4,3,1,2,0:T(8,128)(2,1)S(1)}, u32[]{:S(2)}, u32[]{:S(2)}) %all-to-all-start.1) | async-done | bytes 524320 | tf_op jit(solution)/shard_map/all_to_all | solution.py:42
  144.9 0.9 fusion.44
  (10 shorter events, 0.0 us)
Async XLA Ops:
  6.5 46.3 %all-gather.2.cloned.1.call-start = ((), (), s32[]{:S(2)}) async-start(), calls=%async_computation.2 | async-start | bytes 2621440 | tf_op jit(solution)/shard_map/all_gather | solution.py:30
  31.1 91.5 %all-reduce.3.cloned.1.call-start = ((), (), s32[]{:S(2)}) async-start(), calls=%async_computation.3 | async-start | bytes 4194304
  52.8 6.5 %copy-start.2 = (bf16[8,4,1,8,4096]{4,3,1,0,2:T(8,128)(2,1)S(1)}, bf16[8,4,1,8,4096]{4,3,1,0,2:T(8,128)(2,1)}, u32[]{:S(2)}) copy-start(bf16[8,4,1,8,4096]{4,3,1,0,2:T(8,128)(2,1)} %all-gather.2.cloned.1.call-done) | copy-start | bytes 6291460
  59.3 11.7 %copy-start.3 = (u32[32]{0:T(128)S(1)}, u32[32]{0:T(128)}, u32[]{:S(2)}) copy-start(u32[32]{0:T(128)} %constant.21) | copy-start | bytes 388
  59.4 71.4 %copy-start = (s32[16,2]{0,1:T(2,128)S(1)}, s32[16,2]{0,1:T(2,128)}, u32[]{:S(2)}) copy-start(s32[16,2]{0,1:T(2,128)} %param.7) | copy-start | bytes 388
  59.4 85.5 %copy-start.1 = (f32[16,2]{0,1:T(2,128)S(1)}, f32[16,2]{0,1:T(2,128)}, u32[]{:S(2)}) copy-start(f32[16,2]{0,1:T(2,128)} %param.8) | copy-start | bytes 388
  125.1 19.8 %all-to-all-start.1 = ((bf16[8,1,1,8,4096]{4,3,1,2,0:T(8,128)(2,1)}), bf16[8,1,1,8,4096]{4,3,1,2,0:T(8,128)(2,1)S(1)}, u32[]{:S(2)}, u32[]{:S(2)}) async-start(bf16[8,1,1,8,4096]{4,3,1,2,0:T(8,128)(2,1)} %dynamic-slice_bitcast_fusion), calls=%async_computation.1 | async-start | bytes 1048576 | tf_op jit(solution)/shard_map/all_to_all | solution.py:42
Sparse Core Ops, SparseCore 0:
  31.2 21.5 all-gather.1
  71.2 51.3 all-reduce.2
where the time goes:
time: 153 us
  waiting for transfers between devices  86.7 us (57%)
  blocking collectives  21.7 us (14%)
  matrix products  19.5 us (13%)
  between operations  13.5 us (9%)
  starting transfers between devices  5.56 us (4%)
  local copies, waits for them, and re-layouts  5.33 us (3%)
    unnamed x3, waiting for transfers between devices  51 us
    all_to_all x1, blocking collectives, body(): lax.all_to_all(shaped, 'ep', split_axis=0, concat_axis=0, tiled=True)  21.7 us
    all_gather x1, waiting for transfers between devices, body(): block_rows = lax.all_gather(arrived, 'tp', axis=1, tiled=True)  21.7 us
    all_to_all x1, waiting for transfers between devices, body(): lax.all_to_all(summed, 'ep', split_axis=0, concat_axis=0, tiled=True)  14.1 us
    dot_general x1, matrix products, body(): jnp.einsum('abecf,efd->abecd', hidden, down_weight, preferred_element_typ...  11.7 us
    dot_general x1, matrix products, body(): jnp.einsum('abecd,edf->abecf', block_rows, gate_weight, preferred_element...  6.49 us
    all_to_all x1, starting transfers between devices, body(): lax.all_to_all(summed, 'ep', split_axis=0, concat_axis=0, tiled=True)  5.52 us
  transfers between devices with their start and end apart: 3, of which 3 were waited for; matrix products, arithmetic and copies ran while one was open for 0% of the time, Pallas kernels for 0%

commit v1 on v0

--- a/solution.py
+++ b/solution.py
@@ -27,7 +27,13 @@
     ).astype(jnp.bfloat16)
     shaped = buffer.reshape(rank_count, 1, experts_here, capacity, feature_width)
     arrived = lax.all_to_all(shaped, "ep", split_axis=0, concat_axis=0, tiled=True)
-    block_rows = lax.all_gather(arrived, "tp", axis=1, tiled=True)
+    n_dev = lax.axis_size("tp")
+    current, blocks = (arrived, [arrived])
+    for _ in range(n_dev - 1):
+        current = lax.ppermute(current, "tp", [(i, (i + 1) % n_dev) for i in range(n_dev)])
+        blocks.insert(0, current)
+    line = jnp.concatenate(blocks, axis=1)
+    block_rows = jnp.roll(line, (lax.axis_index("tp") + 1) * arrived.shape[1], axis=1)
     gate_values = jnp.einsum(
         "abecd,edf->abecf", block_rows, gate_weight, preferred_element_type=jnp.float32
     )

time: 153 us -> 158 us (1.033)
  waiting for transfers between devices: 86.7 us -> 89.9 us
  local copies, waits for them, and re-layouts: 5.33 us -> 7.54 us
    ppermute x0 -> x3, waiting for transfers between devices: none -> 25.8 us  [body(): lax.ppermute(current, 'tp', [(i, (i + 1) % n_dev) for i in range(n_dev)])]
    all_gather x1 -> x0, waiting for transfers between devices: 21.7 us -> none  [body(): block_rows = lax.all_gather(arrived, 'tp', axis=1, tiled=True)]
    unnamed x10 -> x17, local copies, waits for them, and re-layouts: 1.36 us -> 3.54 us
    unnamed x3 -> x2, waiting for transfers between devices: 51 us -> 50 us
  transfers between devices with their start and end apart: 3 -> 5, of which waited for: 3 -> 5; matrix products, arithmetic and copies ran while one was open for 0% -> 0% of each run, Pallas kernels for 0% -> 0%
where the time goes in v1:
time: 158 us
  waiting for transfers between devices  89.9 us (57%)
  blocking collectives  21.6 us (14%)
  matrix products  19.4 us (12%)
  between operations  13.5 us (9%)
  local copies, waits for them, and re-layouts  7.54 us (5%)
  starting transfers between devices  5.53 us (4%)
    unnamed x2, waiting for transfers between devices  50 us
    ppermute x3, waiting for transfers between devices, body(): lax.ppermute(current, 'tp', [(i, (i + 1) % n_dev) for i in range(n_dev)])  25.8 us
    all_to_all x1, blocking collectives, body(): lax.all_to_all(shaped, 'ep', split_axis=0, concat_axis=0, tiled=True)  21.6 us
    all_to_all x1, waiting for transfers between devices, body(): lax.all_to_all(summed, 'ep', split_axis=0, concat_axis=0, tiled=True)  14.1 us
    dot_general x1, matrix products, body(): jnp.einsum('abecf,efd->abecd', hidden, down_weight, preferred_element_typ...  12.3 us
    dot_general x1, matrix products, body(): jnp.einsum('abecd,edf->abecf', block_rows, gate_weight, preferred_element...  5.78 us
    all_to_all x1, starting transfers between devices, body(): lax.all_to_all(summed, 'ep', split_axis=0, concat_axis=0, tiled=True)  5.52 us
    unnamed x17, local copies, waits for them, and re-layouts  3.54 us
  transfers between devices with their start and end apart: 5, of which 5 were waited for; matrix products, arithmetic and copies ran while one was open for 0% of the time, Pallas kernels for 0%

profile of v1, /device:TPU:0, one launch (start us, length us, event | category | flops | bytes accessed | tf_op | source)
XLA Modules:
  0.0 157.8 jit_solution(14847909438469543599)
XLA Ops:
  6.5 0.8 copy.23
  7.3 0.1 eq.53
  7.4 0.1 fusion.38
  7.5 0.1 reduce_window_sum.11
  7.5 0.2 select_reduce_fusion
  7.7 1.1 broadcast_in_dim.2
  8.8 0.1 reshape.65
  8.9 0.4 fusion.12
  9.3 21.6 %all_to_all.10 = bf16[8,1,1,8,4096]{4,3,2,1,0:T(8,128)(2,1)S(1)} all-to-all(bf16[8,1,1,8,4096]{4,3,2,1,0:T(8,128)(2,1)S(1)} %fusion.12), channel_id=1, replica_groups=mesh['ep'=8,'tp'=4] {'ep'}, dimensions={0} | all-to-all | bytes 1048576 | tf_op jit(solution)/shard_map/all_to_all | solution.py:29
  31.0 8.6 %collective-permute-done = bf16[8,1,1,8,4096]{4,3,2,1,0:T(8,128)(2,1)S(1)} collective-permute-done((bf16[8,1,1,8,4096]{4,3,2,1,0:T(8,128)(2,1)S(1)}, bf16[8,1,1,8,4096]{4,3,2,1,0:T(8,128)(2,1)S(1)}, u32[]{:S(2)}, u32[]{:S(2)}) %collective-permute-start) | collective-permute-done | bytes 524320 | tf_op jit(solution)/shard_map/ppermute | solution.py:33
  39.6 8.6 %collective-permute-done.1 = bf16[8,1,1,8,4096]{4,3,2,1,0:T(8,128)(2,1)S(1)} collective-permute-done((bf16[8,1,1,8,4096]{4,3,2,1,0:T(8,128)(2,1)S(1)}, bf16[8,1,1,8,4096]{4,3,2,1,0:T(8,128)(2,1)S(1)}, u32[]{:S(2)}, u32[]{:S(2)}) %collective-permute-start.1) | collective-permute-done | bytes 524320 | tf_op jit(solution)/shard_map/ppermute | solution.py:33
  48.2 8.6 %collective-permute-done.2 = bf16[8,1,1,8,4096]{4,3,2,1,0:T(8,128)(2,1)S(1)} collective-permute-done((bf16[8,1,1,8,4096]{4,3,2,1,0:T(8,128)(2,1)S(1)}, bf16[8,1,1,8,4096]{4,3,2,1,0:T(8,128)(2,1)S(1)}, u32[]{:S(2)}, u32[]{:S(2)}) %collective-permute-start.2) | collective-permute-done | bytes 524320 | tf_op jit(solution)/shard_map/ppermute | solution.py:33
  57.2 1.9 %copy-done = bf16[8,8,1,8,4096]{4,3,2,1,0:T(8,128)(2,1)} copy-done((bf16[8,8,1,8,4096]{4,3,2,1,0:T(8,128)(2,1)}, bf16[8,8,1,8,4096]{4,3,2,1,0:T(8,128)(2,1)S(1)}, u32[]{:S(2)}) %copy-start) | copy-done | bytes 4194328
  59.1 5.8 %fusion.17 = f32[8,4,1,8,1024]{4,3,1,0,2:T(8,128)S(1)} fusion(bf16[1,4096,1024]{2,1,0:T(8,128)(2,1)} %param.9, bf16[8,8,1,8,4096]{4,3,2,1,0:T(8,128)(2,1)S(1)} %constant_dynamic-update-slice_fusion, s32[]{:T(128)S(6)} %select_n.14), kind=kOutput, calls=%fused_computation.15 | convolution fusion | flops 2147483648 | bytes 11534340 | tf_op jit(solution)/shard_map/abecd,edf->abecf/dot_general | solution.py:37
  64.9 12.3 %fusion.9 = bf16[8,4,1,8,4096]{4,3,1,0,2:T(8,128)(2,1)} fusion(bf16[1,1024,4096]{2,1,0:T(8,128)(2,1)} %param.11, f32[8,4,1,8,1024]{4,3,1,0,2:T(8,128)S(1)} %fusion.17, bf16[1,4096,1024]{2,1,0:T(8,128)(2,1)} %param.10, bf16[8,8,1,8,4096]{4,3,2,1,0:T(8,128)(2,1)} %copy-done, s32[]{:T(128)S(6)} %select_n.14), kind=kOutput, calls=%fused_computation.7 | convolution fusion | flops 4297588736 | bytes 22020100 | tf_op jit(solution)/shard_map/abecf,efd->abecd/dot_general | solution.py:44
  77.2 0.0 all-reduce.3.cloned.1.call-update
  77.2 0.6 dynamic-slice
  77.8 49.9 %all-reduce.3.cloned.1.call-done = bf16[8,4,1,8,4096]{4,3,1,0,2:T(8,128)(2,1)} async-done(((bf16[8,4,1,8,4096]{4,3,1,0,2:T(8,128)(2,1)}), bf16[8,4,1,8,4096]{4,3,1,0,2:T(8,128)(2,1)}) %all-reduce.3.cloned.1.call-update) | async-done | bytes 2097168
  127.7 2.5 %dynamic-slice_bitcast_fusion = bf16[8,1,1,8,4096]{4,3,1,2,0:T(8,128)(2,1)} fusion(bf16[8,4,1,8,4096]{4,3,1,0,2:T(8,128)(2,1)} %all-reduce.3.cloned.1.call-done, u32[]{:T(128)} %bitcast.43), kind=kLoop, calls=%fused_computation.20 | loop fusion | bytes 1048580 | tf_op jit(solution)/shard_map/reduce_scatter | solution.py:47
  130.2 5.5 %all-to-all-start.1 = ((bf16[8,1,1,8,4096]{4,3,1,2,0:T(8,128)(2,1)}), bf16[8,1,1,8,4096]{4,3,1,2,0:T(8,128)(2,1)S(1)}, u32[]{:S(2)}, u32[]{:S(2)}) async-start(bf16[8,1,1,8,4096]{4,3,1,2,0:T(8,128)(2,1)} %dynamic-slice_bitcast_fusion), calls=%async_computation.1 | async-start | bytes 1048576 | tf_op jit(solution)/shard_map/all_to_all | solution.py:48
  135.8 0.1 reduce_sum.21
  135.8 0.1 copy.24
  135.9 14.1 %all-to-all-done.1 = bf16[8,1,1,8,4096]{4,3,1,2,0:T(8,128)(2,1)S(1)} async-done(((bf16[8,1,1,8,4096]{4,3,1,2,0:T(8,128)(2,1)}), bf16[8,1,1,8,4096]{4,3,1,2,0:T(8,128)(2,1)S(1)}, u32[]{:S(2)}, u32[]{:S(2)}) %all-to-all-start.1) | async-done | bytes 524320 | tf_op jit(solution)/shard_map/all_to_all | solution.py:48
  150.0 0.9 fusion.27
  (21 shorter events, 0.3 us)
Async XLA Ops:
  6.5 121.2 %all-reduce.3.cloned.1.call-start = ((), (), s32[]{:S(2)}) async-start(), calls=%async_computation.2 | async-start | bytes 4194304
  31.0 8.6 %collective-permute-start = (bf16[8,1,1,8,4096]{4,3,2,1,0:T(8,128)(2,1)S(1)}, bf16[8,1,1,8,4096]{4,3,2,1,0:T(8,128)(2,1)S(1)}, u32[]{:S(2)}, u32[]{:S(2)}) collective-permute-start(bf16[8,1,1,8,4096]{4,3,2,1,0:T(8,128)(2,1)S(1)} %all_to_all.10), channel_id=1, source_target_pairs={{0,1},{1,2},{2,3},{3,0},{4,5},{5,6},{6,7},{7,4},{8,9},{9,10},{10,1... | collective-permute-start | bytes 1572872 | tf_op jit(solution)/shard_map/ppermute | solution.py:33
  39.6 8.6 %collective-permute-start.1 = (bf16[8,1,1,8,4096]{4,3,2,1,0:T(8,128)(2,1)S(1)}, bf16[8,1,1,8,4096]{4,3,2,1,0:T(8,128)(2,1)S(1)}, u32[]{:S(2)}, u32[]{:S(2)}) collective-permute-start(bf16[8,1,1,8,4096]{4,3,2,1,0:T(8,128)(2,1)S(1)} %collective-permute-done), channel_id=1, source_target_pairs={{0,1},{1,2},{2,3},{3,0},{4,5},{5,6},{6,7},{7,4},{8,9},{9,10},{10,1... | collective-permute-start | bytes 1572872 | tf_op jit(solution)/shard_map/ppermute | solution.py:33
  48.2 8.6 %collective-permute-start.2 = (bf16[8,1,1,8,4096]{4,3,2,1,0:T(8,128)(2,1)S(1)}, bf16[8,1,1,8,4096]{4,3,2,1,0:T(8,128)(2,1)S(1)}, u32[]{:S(2)}, u32[]{:S(2)}) collective-permute-start(bf16[8,1,1,8,4096]{4,3,2,1,0:T(8,128)(2,1)S(1)} %collective-permute-done.1), channel_id=1, source_target_pairs={{0,1},{1,2},{2,3},{3,0},{4,5},{5,6},{6,7},{7,4},{8,9},{9,10},{10,1... | collective-permute-start | bytes 1572872 | tf_op jit(solution)/shard_map/ppermute | solution.py:33
  57.2 1.9 %copy-start = (bf16[8,8,1,8,4096]{4,3,2,1,0:T(8,128)(2,1)}, bf16[8,8,1,8,4096]{4,3,2,1,0:T(8,128)(2,1)S(1)}, u32[]{:S(2)}) copy-start(bf16[8,8,1,8,4096]{4,3,2,1,0:T(8,128)(2,1)S(1)} %constant_dynamic-update-slice_fusion) | copy-start | bytes 12582916
  64.9 12.3 %copy-start.3 = (u32[32]{0:T(128)S(1)}, u32[32]{0:T(128)}, u32[]{:S(2)}) copy-start(u32[32]{0:T(128)} %constant.48) | copy-start | bytes 388
  77.2 58.8 %copy-start.1 = (s32[16,2]{0,1:T(2,128)S(1)}, s32[16,2]{0,1:T(2,128)}, u32[]{:S(2)}) copy-start(s32[16,2]{0,1:T(2,128)} %param.7) | copy-start | bytes 388
  77.2 72.9 %copy-start.2 = (f32[16,2]{0,1:T(2,128)S(1)}, f32[16,2]{0,1:T(2,128)}, u32[]{:S(2)}) copy-start(f32[16,2]{0,1:T(2,128)} %param.8) | copy-start | bytes 388
  130.2 19.8 %all-to-all-start.1 = ((bf16[8,1,1,8,4096]{4,3,1,2,0:T(8,128)(2,1)}), bf16[8,1,1,8,4096]{4,3,1,2,0:T(8,128)(2,1)S(1)}, u32[]{:S(2)}, u32[]{:S(2)}) async-start(bf16[8,1,1,8,4096]{4,3,1,2,0:T(8,128)(2,1)} %dynamic-slice_bitcast_fusion), calls=%async_computation.1 | async-start | bytes 1048576 | tf_op jit(solution)/shard_map/all_to_all | solution.py:48
Sparse Core Ops, SparseCore 0:
  77.3 50.3 all-reduce.2
